TPU v7x, 64 devices: a 2x2x8 block of a 4x4x8 slice. The times are simulated.
64 devices in a mesh: mol: 4 (over x, y), occ: 16 (over z, core).
Axes of the slice: x: 2, y: 2, z: 8, core: 2. Of those that a mesh axis runs over, the one named last changes fastest.
The devices are a block of a 4x4x8 slice.
Arguments:
- b_ints: bfloat16 [64, 672, 32, 160], P('mol', None, 'occ'), parts along dimension 0
- eps_occ: float32 [64, 32], P('mol'), parts along dimension 0
- eps_vir: float32 [64, 160], P('mol'), parts along dimension 0
- active: int32 [64, 32], P('mol'), parts along dimension 0
Outputs:
- output 1: float32 [64, 32], P('mol', 'occ'), parts along dimension 0
- output 2: float32 [64], P('mol'), parts along dimension 0
There are 4 independent parts. A program takes and returns all parts, laid end to end along the dimension named above; each array names one.
All inputs are finite; a program needn't handle non-finite values.
Results may differ from a plain program's by a relative error of at most 0.001.
Values are sent between devices in bfloat16 or wider.
A program may use at most 768 MiB of HBM per device.

v0:
```python
import jax
import jax.numpy as jnp
from jax import lax
from jax.sharding import PartitionSpec as P


def pair_block(x_blk, y_blk, eps_x, eps_y, act_x, act_y, eps_vir):
    vir_sum = eps_vir[:, :, None, None] + eps_vir[:, None, None, :]

    def row_energy(row_idx):
        x_row = lax.dynamic_index_in_dim(x_blk, row_idx, axis=2, keepdims=False)
        k_pair = jnp.einsum("fqa,fqjb->fajb", x_row, y_blk, preferred_element_type=jnp.float32)
        eps_row = lax.dynamic_index_in_dim(eps_x, row_idx, axis=1, keepdims=True)
        denominator = eps_row[:, :, None, None] + eps_y[:, None, :, None] - vir_sum
        pair_terms = k_pair * (2.0 * k_pair - jnp.transpose(k_pair, (0, 3, 2, 1))) / denominator
        return jnp.sum(pair_terms, axis=(1, 3))

    row_sums = lax.map(row_energy, jnp.arange(x_blk.shape[2]))
    return jnp.transpose(row_sums, (1, 0, 2)) * act_x[:, :, None] * act_y[:, None, :]


def solution(mesh):
    n_dev = mesh.shape["occ"]
    shift_perm = [(src_dev, (src_dev + 1) % n_dev) for src_dev in range(n_dev)]
    n_full = (n_dev - 1) // 2
    has_mid = n_dev % 2 == 0

    def local_fn(b_own, eps_occ, eps_vir, active):
        n_loc = b_own.shape[2]
        half_n = n_loc // 2
        my_index = lax.axis_index("occ")
        act_all = active.astype(jnp.float32)

        def block_of(values, owner_idx):
            return lax.dynamic_slice_in_dim(values, owner_idx * n_loc, n_loc, axis=1)

        def add_credit(credit, owner_idx, values):
            start_col = owner_idx * n_loc
            prior_val = lax.dynamic_slice_in_dim(credit, start_col, n_loc, axis=1)
            return lax.dynamic_update_slice_in_dim(credit, prior_val + values, start_col, axis=1)

        eps_own = block_of(eps_occ, my_index)
        act_own = block_of(act_all, my_index)
        own_sum = jnp.sum(pair_block(b_own, b_own, eps_own, eps_own, act_own, act_own, eps_vir), axis=2)
        credit_all = jnp.zeros(eps_occ.shape, jnp.float32)
        visiting = b_own
        for step_idx in range(1, n_full + 1):
            visiting = lax.ppermute(visiting, "occ", shift_perm)
            vis_owner = (my_index - step_idx) % n_dev
            pair_e = pair_block(b_own, visiting, eps_own, block_of(eps_occ, vis_owner), act_own, block_of(act_all, vis_owner), eps_vir)
            own_sum = own_sum + jnp.sum(pair_e, axis=2)
            credit_all = add_credit(credit_all, vis_owner, jnp.sum(pair_e, axis=1))
        if has_mid:
            visiting = lax.ppermute(visiting, "occ", shift_perm)
            vis_owner = (my_index + n_dev // 2) % n_dev
            eps_vis = block_of(eps_occ, vis_owner)
            act_vis = block_of(act_all, vis_owner)

            def lower_half(b_vis):
                pair_e = pair_block(b_own[:, :, :half_n], b_vis, eps_own[:, :half_n], eps_vis, act_own[:, :half_n], act_vis, eps_vir)
                row_part = jnp.sum(pair_e, axis=2)
                zero_pad = jnp.zeros((row_part.shape[0], n_loc - half_n), jnp.float32)
                return jnp.concatenate([row_part, zero_pad], axis=1), jnp.sum(pair_e, axis=1)

            def upper_half(b_vis):
                pair_e = pair_block(b_own, b_vis[:, :, half_n:], eps_own, eps_vis[:, half_n:], act_own, act_vis[:, half_n:], eps_vir)
                col_part = jnp.sum(pair_e, axis=1)
                zero_pad = jnp.zeros((col_part.shape[0], half_n), jnp.float32)
                return jnp.sum(pair_e, axis=2), jnp.concatenate([zero_pad, col_part], axis=1)

            mid_own, mid_credit = lax.cond(my_index < n_dev // 2, lower_half, upper_half, visiting)
            own_sum = own_sum + mid_own
            credit_all = add_credit(credit_all, vis_owner, mid_credit)
        returned = lax.psum_scatter(credit_all, "occ", scatter_dimension=1, tiled=True)
        e_pair = own_sum + returned
        energy = lax.psum(jnp.sum(e_pair, axis=1), "occ")
        return e_pair, energy

    return jax.shard_map(local_fn, mesh=mesh, in_specs=(P("mol", None, "occ", None), P("mol", None), P("mol", None), P("mol", None)), out_specs=(P("mol", "occ"), P("mol")), check_vma=False)
```

profile of v0, /device:TPU:21, one launch (start us, length us, event | category | flops | bytes accessed | tf_op | source)
XLA Modules:
  0.0 858.3 jit_solution(3020081414739150694)
XLA Ops:
  3.8 84.8 %collective-permute-done = bf16[16,672,2,160]{1,3,2,0:T(8,128)(2,1)S(1)} collective-permute-done((bf16[16,672,2,160]{1,3,2,0:T(8,128)(2,1)}, bf16[16,672,2,160]{1,3,2,0:T(8,128)(2,1)S(1)}, u32[]{:S(2)}, u32[]{:S(2)}) %collective-permute-start) | collective-permute-done | bytes 6881312 | tf_op jit(solution)/shard_map/ppermute | solution.py:48
  91.1 84.8 %collective-permute-done.1 = bf16[16,672,2,160]{1,3,2,0:T(8,128)(2,1)S(1)} collective-permute-done((bf16[16,672,2,160]{1,3,2,0:T(8,128)(2,1)S(1)}, bf16[16,672,2,160]{1,3,2,0:T(8,128)(2,1)S(1)}, u32[]{:S(2)}, u32[]{:S(2)}) %collective-permute-start.1) | collective-permute-done | bytes 6881312 | tf_op jit(solution)/shard_map/ppermute | solution.py:48
  181.5 84.8 %collective-permute-done.2 = bf16[16,672,2,160]{1,3,2,0:T(8,128)(2,1)} collective-permute-done((bf16[16,672,2,160]{1,3,2,0:T(8,128)(2,1)S(1)}, bf16[16,672,2,160]{1,3,2,0:T(8,128)(2,1)}, u32[]{:S(2)}, u32[]{:S(2)}) %collective-permute-start.2) | collective-permute-done | bytes 6881312 | tf_op jit(solution)/shard_map/ppermute | solution.py:48
  270.5 83.0 %collective-permute-done.3 = bf16[16,672,2,160]{1,3,2,0:T(8,128)(2,1)} collective-permute-done((bf16[16,672,2,160]{1,3,2,0:T(8,128)(2,1)}, bf16[16,672,2,160]{1,3,2,0:T(8,128)(2,1)}, u32[]{:S(2)}, u32[]{:S(2)}) %collective-permute-start.3) | collective-permute-done | bytes 6881312 | tf_op jit(solution)/shard_map/ppermute | solution.py:48
  356.0 48.3 %while.103 = (s32[]{:T(128)}, f32[2,16,2]{1,2,0:T(2,128)S(1)}, s32[2]{0:T(128)S(1)}, bf16[16,672,2,160]{1,3,2,0:T(8,128)(2,1)}, f32[16,2]{0,1:T(2,128)S(1)}, /*i...) while((s32[]{:T(128)}, f32[2,16,2]{1,2,0:T(2,128)S(1)}, s32[2]{0:T(128)S(1)}, ...), condition=%wide.region_2.3_spmd.clone, body=%wide.region_0.2_spmd.clone.sunk | while | flops 1106329600 | bytes 31470944 | solution.py:18
  359.8 9.0 %fusion.188 = f32[16,160,2,160]{3,1,2,0:T(8,128)} fusion(bf16[16,672,2,160]{1,3,2,0:T(8,128)(2,1)} %get-tuple-element.1660, s32[]{:T(128)S(6)} %select_n.164), kind=kOutput, calls=%fused_computation.43.clone.1 | convolution fusion | flops 1101004800 | bytes 15073284 | tf_op jit(solution)/shard_map/while/body/eval_jaxpr/fqa,fqjb->fajb/dot_general | solution.py:12
  384.0 9.0 %fusion.188 = f32[16,160,2,160]{3,1,2,0:T(8,128)} fusion(bf16[16,672,2,160]{1,3,2,0:T(8,128)(2,1)} %get-tuple-element.1660, s32[]{:T(128)S(6)} %select_n.164), kind=kOutput, calls=%fused_computation.43.clone.1 | convolution fusion | flops 1101004800 | bytes 15073284 | tf_op jit(solution)/shard_map/while/body/eval_jaxpr/fqa,fqjb->fajb/dot_general | solution.py:12
  418.5 46.6 %while.104 = (s32[]{:T(128)}, f32[2,16,2]{1,2,0:T(2,128)S(1)}, s32[2]{0:T(128)S(1)}, bf16[16,672,2,160]{1,3,0,2:T(8,128)(2,1)}, bf16[16,672,2,160]{1,3,2,0:T(8,1...) while((s32[]{:T(128)}, f32[2,16,2]{1,2,0:T(2,128)S(1)}, ...), condition=%wide.region_6.7_spmd.clone, body=%wide.region_4.6_spmd.clone.sunk | while | flops 1106329600 | bytes 31470704 | solution.py:18
  421.5 8.9 %fusion.193 = f32[16,160,2,160]{3,1,2,0:T(8,128)} fusion(bf16[16,672,2,160]{1,3,2,0:T(8,128)(2,1)} %get-tuple-element.1434, bf16[16,672,2,160]{1,3,0,2:T(8,128)(2,1)} %get-tuple-element.1433, s32[]{:T(128)S(6)} %select_n.165), kind=kOutput, calls=%fused_computation.56.clone.1 | convolution fusion | flops 1101004800 | bytes 15073284 | tf_op jit(solution)/shard_map/while/body/eval_jaxpr/fqa,fqjb->fajb/dot_general | solution.py:12
  444.9 8.9 %fusion.193 = f32[16,160,2,160]{3,1,2,0:T(8,128)} fusion(bf16[16,672,2,160]{1,3,2,0:T(8,128)(2,1)} %get-tuple-element.1434, bf16[16,672,2,160]{1,3,0,2:T(8,128)(2,1)} %get-tuple-element.1433, s32[]{:T(128)S(6)} %select_n.165), kind=kOutput, calls=%fused_computation.56.clone.1 | convolution fusion | flops 1101004800 | bytes 15073284 | tf_op jit(solution)/shard_map/while/body/eval_jaxpr/fqa,fqjb->fajb/dot_general | solution.py:12
  465.7 46.7 %while.105 = (s32[]{:T(128)}, f32[2,16,2]{1,2,0:T(2,128)S(1)}, s32[2]{0:T(128)S(1)}, bf16[16,672,2,160]{1,3,0,2:T(8,128)(2,1)}, bf16[16,672,2,160]{1,3,2,0:T(8,1...) while((s32[]{:T(128)}, f32[2,16,2]{1,2,0:T(2,128)S(1)}, ...), condition=%wide.region_10.11_spmd.clone, body=%wide.region_8.10_spmd.clone.sunk | while | flops 1106329600 | bytes 31470704 | solution.py:18
  513.0 46.6 %while.106 = (s32[]{:T(128)}, f32[2,16,2]{1,2,0:T(2,128)S(1)}, s32[2]{0:T(128)S(1)}, bf16[16,672,2,160]{1,3,0,2:T(8,128)(2,1)}, bf16[16,672,2,160]{1,3,2,0:T(8,1...) while((s32[]{:T(128)}, f32[2,16,2]{1,2,0:T(2,128)S(1)}, ...), condition=%wide.region_14.15_spmd.clone, body=%wide.region_12.14_spmd.clone.sunk | while | flops 1106329600 | bytes 31470704 | solution.py:18
  516.0 9.0 %fusion.203 = f32[16,160,2,160]{3,1,2,0:T(8,128)} fusion(bf16[16,672,2,160]{1,3,2,0:T(8,128)(2,1)} %get-tuple-element.1500, bf16[16,672,2,160]{1,3,0,2:T(8,128)(2,1)} %get-tuple-element.1499, s32[]{:T(128)S(6)} %select_n.167), kind=kOutput, calls=%fused_computation.82.clone.1 | convolution fusion | flops 1101004800 | bytes 15073284 | tf_op jit(solution)/shard_map/while/body/eval_jaxpr/fqa,fqjb->fajb/dot_general | solution.py:12
  539.3 9.0 %fusion.203 = f32[16,160,2,160]{3,1,2,0:T(8,128)} fusion(bf16[16,672,2,160]{1,3,2,0:T(8,128)(2,1)} %get-tuple-element.1500, bf16[16,672,2,160]{1,3,0,2:T(8,128)(2,1)} %get-tuple-element.1499, s32[]{:T(128)S(6)} %select_n.167), kind=kOutput, calls=%fused_computation.82.clone.1 | convolution fusion | flops 1101004800 | bytes 15073284 | tf_op jit(solution)/shard_map/while/body/eval_jaxpr/fqa,fqjb->fajb/dot_general | solution.py:12
  561.3 46.6 %while.107 = (s32[]{:T(128)}, f32[2,16,2]{1,2,0:T(2,128)S(1)}, s32[2]{0:T(128)S(1)}, bf16[16,672,2,160]{1,3,0,2:T(8,128)(2,1)}, bf16[16,672,2,160]{1,3,2,0:T(8,1...) while((s32[]{:T(128)}, f32[2,16,2]{1,2,0:T(2,128)S(1)}, ...), condition=%wide.region_18.19_spmd.clone, body=%wide.region_16.18_spmd.clone.sunk | while | flops 1106329600 | bytes 31470704 | solution.py:18
  564.4 9.0 %fusion.208 = f32[16,160,2,160]{3,1,2,0:T(8,128)} fusion(bf16[16,672,2,160]{1,3,2,0:T(8,128)(2,1)} %get-tuple-element.1533, bf16[16,672,2,160]{1,3,0,2:T(8,128)(2,1)} %get-tuple-element.1532, s32[]{:T(128)S(6)} %select_n.168), kind=kOutput, calls=%fused_computation.95.clone.1 | convolution fusion | flops 1101004800 | bytes 15073284 | tf_op jit(solution)/shard_map/while/body/eval_jaxpr/fqa,fqjb->fajb/dot_general | solution.py:12
  587.7 9.0 %fusion.208 = f32[16,160,2,160]{3,1,2,0:T(8,128)} fusion(bf16[16,672,2,160]{1,3,2,0:T(8,128)(2,1)} %get-tuple-element.1533, bf16[16,672,2,160]{1,3,0,2:T(8,128)(2,1)} %get-tuple-element.1532, s32[]{:T(128)S(6)} %select_n.168), kind=kOutput, calls=%fused_computation.95.clone.1 | convolution fusion | flops 1101004800 | bytes 15073284 | tf_op jit(solution)/shard_map/while/body/eval_jaxpr/fqa,fqjb->fajb/dot_general | solution.py:12
  608.5 46.8 %while.108 = (s32[]{:T(128)}, f32[2,16,2]{1,2,0:T(2,128)S(1)}, s32[2]{0:T(128)S(1)}, bf16[16,672,2,160]{1,3,0,2:T(8,128)(2,1)}, bf16[16,672,2,160]{1,3,2,0:T(8,1...) while((s32[]{:T(128)}, f32[2,16,2]{1,2,0:T(2,128)S(1)}, ...), condition=%wide.region_22.23_spmd.clone, body=%wide.region_20.22_spmd.clone.sunk | while | flops 1106329600 | bytes 31470704 | solution.py:18
  655.9 46.6 %while.109 = (s32[]{:T(128)}, f32[2,16,2]{1,2,0:T(2,128)S(1)}, s32[2]{0:T(128)S(1)}, bf16[16,672,2,160]{1,3,0,2:T(8,128)(2,1)}, bf16[16,672,2,160]{1,3,2,0:T(8,1...) while((s32[]{:T(128)}, f32[2,16,2]{1,2,0:T(2,128)S(1)}, ...), condition=%wide.region_26.27_spmd.clone, body=%wide.region_24.26_spmd.clone.sunk | while | flops 1106329600 | bytes 31470704 | solution.py:18
  702.6 46.7 %while.110 = (s32[]{:T(128)}, f32[2,16,2]{1,2,0:T(2,128)S(1)}, s32[2]{0:T(128)S(1)}, bf16[16,672,2,160]{1,3,0,2:T(8,128)(2,1)}, bf16[16,672,2,160]{1,3,2,0:T(8,1...) while((s32[]{:T(128)}, f32[2,16,2]{1,2,0:T(2,128)S(1)}, ...), condition=%wide.region_30.31_spmd.clone, body=%wide.region_28.30_spmd.clone.sunk | while | flops 1106329600 | bytes 31470704 | solution.py:18
  749.7 21.3 %conditional.1 = (f32[16,2]{0,1:T(2,128)S(1)}, f32[16,2]{0,1:T(2,128)S(1)}) conditional(s32[]{:T(128)} %convert_element_type.7, (bf16[16,672,2,160]{1,3,2,0:T(8,128)(2,1)}, f32[16,2]{1,0:T(8,128)S(1)}, f32[16,160]{1,0:T(8,128)S(1)}, bf16[16,672,2,160]{1,3,2,0:T(8,128)(2,1)}, f32[16,2]{0,1:T(2,128)S(1)}, /*index=5*/f32[16,2]{1,0:T(8,128)S(1)}, ...), branch_computations={%region_32.37_spmd, %region_37.40_spmd} | conditional | flops 1106329728 | bytes 36713772 | solution.py:71
  750.5 9.0 %fusion.21 = f32[16,160,2,160]{3,1,2,0:T(8,128)} fusion(bf16[16,672,2,160]{1,3,2,0:T(8,128)(2,1)} %get-tuple-element.417, bf16[16,672,2,160]{1,3,2,0:T(8,128)(2,1)} %get-tuple-element.747), kind=kOutput, calls=%fused_computation.14 | convolution fusion | flops 1101004800 | bytes 15073280 | tf_op jit(solution)/shard_map/cond/branch_1_fun/while/body/eval_jaxpr/fqa,fqjb->fajb/dot_general | solution.py:12
  771.0 59.3 %all-reduce.2 = f32[16,32]{0,1:T(8,128)S(1)} all-reduce(f32[16,32]{0,1:T(8,128)S(1)} %constant_dynamic-update-slice_fusion.1), channel_id=2, replica_groups=mesh['mol'=4,'occ'=16] {'occ'}, use_global_device_ids=true, to_apply=%region_47.48.clone | all-reduce | flops 512 | bytes 4096
  830.9 26.9 %psum.7 = f32[16]{0:T(128)} all-reduce(f32[16]{0:T(128)S(1)} %get-tuple-element.924), channel_id=1, replica_groups=mesh['mol'=4,'occ'=16] {'occ'}, use_global_device_ids=true, to_apply=%region_49.50 | all-reduce | flops 16 | bytes 128 | tf_op jit(solution)/shard_map/psum | solution.py:76
  (265 shorter events, 320.1 us)
Async XLA Ops:
  0.6 88.0 %collective-permute-start = (bf16[16,672,2,160]{1,3,2,0:T(8,128)(2,1)}, bf16[16,672,2,160]{1,3,2,0:T(8,128)(2,1)S(1)}, u32[]{:S(2)}, u32[]{:S(2)}) collective-permute-start(bf16[16,672,2,160]{1,3,2,0:T(8,128)(2,1)} %param.24), channel_id=1, source_target_pairs={{0,1},{1,2},{2,3},{3,4},{4,5},{5,6},{6,7},{7,8},{8,9},{9,10},{10,1... | collective-permute-start | bytes 20643848 | tf_op jit(solution)/shard_map/ppermute | solution.py:48
  88.6 177.7 %copy-start.1 = (bf16[16,672,2,160]{1,3,2,0:T(8,128)(2,1)}, bf16[16,672,2,160]{1,3,2,0:T(8,128)(2,1)S(1)}, u32[]{:S(2)}) copy-start(bf16[16,672,2,160]{1,3,2,0:T(8,128)(2,1)S(1)} %collective-permute-done) | copy-start | bytes 20643844
  88.6 87.3 %collective-permute-start.1 = (bf16[16,672,2,160]{1,3,2,0:T(8,128)(2,1)S(1)}, bf16[16,672,2,160]{1,3,2,0:T(8,128)(2,1)S(1)}, u32[]{:S(2)}, u32[]{:S(2)}) collective-permute-start(bf16[16,672,2,160]{1,3,2,0:T(8,128)(2,1)S(1)} %collective-permute-done), channel_id=1, source_target_pairs={{0,1},{1,2},{2,3},{3,4},{4,5},{5,6},{6,7},{7,8},{8,9},{9,10},{10,1... | collective-permute-start | bytes 20643848 | tf_op jit(solution)/shard_map/ppermute | solution.py:48
  179.0 87.3 %collective-permute-start.2 = (bf16[16,672,2,160]{1,3,2,0:T(8,128)(2,1)S(1)}, bf16[16,672,2,160]{1,3,2,0:T(8,128)(2,1)}, u32[]{:S(2)}, u32[]{:S(2)}) collective-permute-start(bf16[16,672,2,160]{1,3,2,0:T(8,128)(2,1)S(1)} %collective-permute-done.1), channel_id=1, source_target_pairs={{0,1},{1,2},{2,3},{3,4},{4,5},{5,6},{6,7},{7,8},{8,9},{9,10},{10,1... | collective-permute-start | bytes 20643848 | tf_op jit(solution)/shard_map/ppermute | solution.py:48
  266.2 87.3 %collective-permute-start.3 = (bf16[16,672,2,160]{1,3,2,0:T(8,128)(2,1)}, bf16[16,672,2,160]{1,3,2,0:T(8,128)(2,1)}, u32[]{:S(2)}, u32[]{:S(2)}) collective-permute-start(bf16[16,672,2,160]{1,3,2,0:T(8,128)(2,1)} %collective-permute-done.2), channel_id=1, source_target_pairs={{0,1},{1,2},{2,3},{3,4},{4,5},{5,6},{6,7},{7,8},{8,9},{9,10},{10,1... | collective-permute-start | bytes 20643848 | tf_op jit(solution)/shard_map/ppermute | solution.py:48
  353.5 111.6 %collective-permute-start.4 = (bf16[16,672,2,160]{1,3,2,0:T(8,128)(2,1)}, bf16[16,672,2,160]{1,3,2,0:T(8,128)(2,1)}, u32[]{:S(2)}, u32[]{:S(2)}) collective-permute-start(bf16[16,672,2,160]{1,3,2,0:T(8,128)(2,1)} %collective-permute-done.3), channel_id=1, source_target_pairs={{0,1},{1,2},{2,3},{3,4},{4,5},{5,6},{6,7},{7,8},{8,9},{9,10},{10,1... | collective-permute-start | bytes 20643848 | tf_op jit(solution)/shard_map/ppermute | solution.py:48
  465.1 94.5 %collective-permute-start.5 = (bf16[16,672,2,160]{1,3,2,0:T(8,128)(2,1)}, bf16[16,672,2,160]{1,3,2,0:T(8,128)(2,1)}, u32[]{:S(2)}, u32[]{:S(2)}) collective-permute-start(bf16[16,672,2,160]{1,3,2,0:T(8,128)(2,1)} %collective-permute-done.4), channel_id=1, source_target_pairs={{0,1},{1,2},{2,3},{3,4},{4,5},{5,6},{6,7},{7,8},{8,9},{9,10},{10,1... | collective-permute-start | bytes 20643848 | tf_op jit(solution)/shard_map/ppermute | solution.py:48
  465.2 47.2 %copy-start.7 = (f32[16,2]{1,0:T(8,128)S(1)}, f32[16,2]{1,0:T(8,128)}, u32[]{:S(2)}) copy-start(f32[16,2]{1,0:T(8,128)} %get-tuple-element.1480) | copy-start | bytes 388
  512.4 48.9 %copy-start.6 = (f32[16,2]{1,0:T(8,128)S(1)}, f32[16,2]{1,0:T(8,128)}, u32[]{:S(2)}) copy-start(f32[16,2]{1,0:T(8,128)} %get-tuple-element.1513) | copy-start | bytes 388
  559.6 95.7 %collective-permute-start.6 = (bf16[16,672,2,160]{1,3,2,0:T(8,128)(2,1)}, bf16[16,672,2,160]{1,3,2,0:T(8,128)(2,1)}, u32[]{:S(2)}, u32[]{:S(2)}) collective-permute-start(bf16[16,672,2,160]{1,3,2,0:T(8,128)(2,1)} %collective-permute-done.5), channel_id=1, source_target_pairs={{0,1},{1,2},{2,3},{3,4},{4,5},{5,6},{6,7},{7,8},{8,9},{9,10},{10,1... | collective-permute-start | bytes 20643848 | tf_op jit(solution)/shard_map/ppermute | solution.py:48
  608.0 47.9 %copy-start.4 = (f32[16,2]{1,0:T(8,128)S(1)}, f32[16,2]{1,0:T(8,128)}, u32[]{:S(2)}) copy-start(f32[16,2]{1,0:T(8,128)} %get-tuple-element.1579) | copy-start | bytes 388
  655.3 94.3 %collective-permute-start.7 = (bf16[16,672,2,160]{1,3,2,0:T(8,128)(2,1)}, bf16[16,672,2,160]{1,3,2,0:T(8,128)(2,1)}, u32[]{:S(2)}, u32[]{:S(2)}) collective-permute-start(bf16[16,672,2,160]{1,3,2,0:T(8,128)(2,1)} %collective-permute-done.6), channel_id=1, source_target_pairs={{0,1},{1,2},{2,3},{3,4},{4,5},{5,6},{6,7},{7,8},{8,9},{9,10},{10,1... | collective-permute-start | bytes 20643848 | tf_op jit(solution)/shard_map/ppermute | solution.py:54
  702.5 46.9 %copy-start.12 = (f32[16,2]{0,1:T(2,128)S(1)}, f32[16,2]{0,1:T(2,128)}, u32[]{:S(2)}) copy-start(f32[16,2]{0,1:T(2,128)} %copy.53) | copy-start | bytes 388
  702.5 46.8 %copy-start.14 = (f32[2,16,2]{1,2,0:T(2,128)S(1)}, f32[2,16,2]{1,2,0:T(2,128)}, u32[]{:S(2)}) copy-start(f32[2,16,2]{1,2,0:T(2,128)} %copy-done.13) | copy-start | bytes 772
  702.5 46.8 %copy-start.16 = (f32[2,16,2]{1,2,0:T(2,128)S(1)}, f32[2,16,2]{1,2,0:T(2,128)}, u32[]{:S(2)}) copy-start(f32[2,16,2]{1,2,0:T(2,128)} %copy-done.15) | copy-start | bytes 772
  702.5 46.8 %copy-start.18 = (f32[2,16,2]{1,2,0:T(2,128)S(1)}, f32[2,16,2]{1,2,0:T(2,128)}, u32[]{:S(2)}) copy-start(f32[2,16,2]{1,2,0:T(2,128)} %copy-done.17) | copy-start | bytes 772
  702.5 46.8 %copy-start.20 = (f32[2,16,2]{1,2,0:T(2,128)S(1)}, f32[2,16,2]{1,2,0:T(2,128)}, u32[]{:S(2)}) copy-start(f32[2,16,2]{1,2,0:T(2,128)} %copy-done.19) | copy-start | bytes 772
  702.5 46.8 %copy-start.22 = (f32[2,16,2]{1,2,0:T(2,128)S(1)}, f32[2,16,2]{1,2,0:T(2,128)}, u32[]{:S(2)}) copy-start(f32[2,16,2]{1,2,0:T(2,128)} %copy-done.21) | copy-start | bytes 772
  702.5 46.8 %copy-start.24 = (f32[16,2]{0,1:T(2,128)S(1)}, f32[16,2]{0,1:T(2,128)}, u32[]{:S(2)}) copy-start(f32[16,2]{0,1:T(2,128)} %copy.68) | copy-start | bytes 388
  702.5 46.8 %copy-start.25 = (f32[16,2]{0,1:T(2,128)S(1)}, f32[16,2]{0,1:T(2,128)}, u32[]{:S(2)}) copy-start(f32[16,2]{0,1:T(2,128)} %copy.66) | copy-start | bytes 388
  702.5 46.8 %copy-start.26 = (f32[16,2]{0,1:T(2,128)S(1)}, f32[16,2]{0,1:T(2,128)}, u32[]{:S(2)}) copy-start(f32[16,2]{0,1:T(2,128)} %copy.64) | copy-start | bytes 388
  702.6 47.1 %copy-start.9 = (f32[16,2]{1,0:T(8,128)S(1)}, f32[16,2]{1,0:T(8,128)}, u32[]{:S(2)}) copy-start(f32[16,2]{1,0:T(8,128)} %copy-done.8) | copy-start | bytes 388
  702.6 47.1 %copy-start.10 = (f32[16,2]{1,0:T(8,128)S(1)}, f32[16,2]{1,0:T(8,128)}, u32[]{:S(2)}) copy-start(f32[16,2]{1,0:T(8,128)} %get-tuple-element.928) | copy-start | bytes 388
  702.6 47.1 %copy-start.11 = (f32[16,2]{1,0:T(8,128)S(1)}, f32[16,2]{1,0:T(8,128)}, u32[]{:S(2)}) copy-start(f32[16,2]{1,0:T(8,128)} %get-tuple-element.937) | copy-start | bytes 388
  (16 other events, 334.6 us)
where the time goes:
time: 872 us; the launch traced here: 858 us
  waiting for transfers between devices  337 us (39%)
  matrix products  152 us (17%)
  local copies, waits for them, and re-layouts  141 us (16%)
  other arithmetic  92.6 us (11%)
  blocking collectives  86.3 us (10%)
  loops' own time  32.1 us (4%)
  starting transfers between devices  15.6 us (2%)
    ppermute x8, waiting for transfers between devices, local_fn(): visiting = lax.ppermute(visiting, 'occ', shift_perm)  337 us
    dot_general x17, matrix products, row_energy(): jnp.einsum('fqa,fqjb->fajb', x_row, y_blk, preferred_element_type=jnp.flo...  152 us
    dot_general x17, local copies, waits for them, and re-layouts, row_energy(): jnp.einsum('fqa,fqjb->fajb', x_row, y_blk, preferred_element_type=jnp.flo...  109 us
    reduce_sum x17, other arithmetic, row_energy(): return jnp.sum(pair_terms, axis=(1, 3))  82.1 us
    unnamed x1, blocking collectives  59.3 us
    another operation x8, loops' own time, pair_block(): row_sums = lax.map(row_energy, jnp.arange(x_blk.shape[2]))  31.8 us
    psum x1, blocking collectives, local_fn(): energy = lax.psum(jnp.sum(e_pair, axis=1), 'occ')  26.9 us
  transfers between devices with their start and end apart: 8, of which 4 were waited for; matrix products, arithmetic and copies ran while one was open for 42% of the time, Pallas kernels for 0%

commit v1 on v0

v1 whole, which is shorter than its diff:
```python
import functools

import jax
import jax.numpy as jnp
from jax import lax
from jax.experimental import pallas as pl
from jax.experimental.pallas import tpu as pltpu
from jax.sharding import PartitionSpec as P

MESH = pl.DeviceIdType.MESH
CORES = 2
LANES = 128


def offsets(n_chip):
    half = n_chip // 2
    order = [(0, 0), (0, 1)]
    for dist in range(half - 1, 0, -1):
        for core in range(CORES):
            order += [(dist, core), (-dist, core)]
    relayed = [(half, core) for core in range(CORES)]
    return order + relayed


def kernel(n_dev, b_hbm, eps_ref, act_ref, vir_ref, out_ref, local, blocks, rest_out, rest_in, relay, relay_rest, vir_sum, acc, result, eps_slot, act_slot, load_sem, own_sem, send_sem, recv_sem, rest_send_sem, rest_recv_sem, hop_send_sem, hop_recv_sem, hop_rest_send_sem, hop_rest_recv_sem, res_send_sem, res_recv_sem):
    n_chip = n_dev // CORES
    half = n_chip // 2
    order = offsets(n_chip)
    n_loc, n_vir, n_aux = blocks.shape[1:]
    n_main = n_aux // LANES * LANES
    n_rest = n_aux - n_main
    fold = LANES // n_rest
    fold_rows = n_loc * n_vir // fold
    me = lax.axis_index("occ")
    chip, core = me // CORES, me % CORES

    def device(d_chip, d_core):
        return (chip + d_chip + n_chip) % n_chip * CORES + (core + d_core) % CORES

    load = pltpu.make_async_copy(b_hbm, local, load_sem)
    load.start()
    own = pltpu.make_async_copy(b_hbm.at[me], blocks.at[0], own_sem)
    own.start()
    barrier = pltpu.get_barrier_semaphore()
    for step in range(1, n_dev):
        pl.semaphore_signal(barrier, inc=1, device_id={"occ": (me + step) % n_dev}, device_id_type=MESH)

    for slot, (d_chip, d_core) in enumerate(order):
        owner = device(-d_chip, d_core)
        for orb in range(n_loc):
            eps_slot[slot, orb] = eps_ref[me, owner * n_loc + orb]
            act_slot[slot, orb] = act_ref[me, owner * n_loc + orb].astype(jnp.float32)
    vir_row = jnp.broadcast_to(vir_ref[pl.ds(me, 1), :], (n_vir, n_vir))
    vir_sum[...] = vir_row + vir_row.T
    acc[...] = jnp.zeros_like(acc)
    result[...] = jnp.zeros_like(result)
    load.wait()

    def pack(frame, carry):
        tail = local[frame, :, :, n_main:].reshape(n_loc * n_vir, n_rest)
        rest_out[frame] = jnp.concatenate([tail[part * fold_rows:(part + 1) * fold_rows] for part in range(fold)], axis=1)
        return carry

    lax.fori_loop(0, n_dev, pack, 0)
    pl.semaphore_wait(barrier, n_dev - 1)

    def main_copy(slot, target, frame):
        return pltpu.make_async_remote_copy(local.at[frame, :, :, pl.ds(0, n_main)], blocks.at[slot, :, :, pl.ds(0, n_main)], send_sem.at[slot], recv_sem.at[slot], device_id={"occ": target}, device_id_type=MESH)

    def rest_copy(slot, target, frame):
        return pltpu.make_async_remote_copy(rest_out.at[frame], rest_in.at[slot], rest_send_sem.at[slot], rest_recv_sem.at[slot], device_id={"occ": target}, device_id_type=MESH)

    hops = []
    for way, (d_chip, d_core) in enumerate(order[-CORES:]):
        frame = device(d_chip, d_core)
        leg = half // 2 if way == 0 else -(half // 2)
        via = device(leg, 0)
        hop = pltpu.make_async_remote_copy(local.at[frame, :, :, pl.ds(0, n_main)], relay.at[way], hop_send_sem.at[way], hop_recv_sem.at[way], device_id={"occ": via}, device_id_type=MESH)
        hop_rest = pltpu.make_async_remote_copy(rest_out.at[frame], relay_rest.at[way], hop_rest_send_sem.at[way], hop_rest_recv_sem.at[way], device_id={"occ": via}, device_id_type=MESH)
        slot = len(order) - CORES + way
        last = device(leg, d_core)
        onward = pltpu.make_async_remote_copy(relay.at[way], blocks.at[slot, :, :, pl.ds(0, n_main)], send_sem.at[slot], recv_sem.at[slot], device_id={"occ": last}, device_id_type=MESH)
        onward_rest = pltpu.make_async_remote_copy(relay_rest.at[way], rest_in.at[slot], rest_send_sem.at[slot], rest_recv_sem.at[slot], device_id={"occ": last}, device_id_type=MESH)
        hop.start()
        hop_rest.start()
        hops.append((hop, hop_rest, onward, onward_rest))
    for slot in range(1, len(order) - CORES):
        target = device(*order[slot])
        rest_copy(slot, target, target).start()
        main_copy(slot, target, target).start()

    own.wait()

    def energy(k_pair, eps_pair):
        terms = k_pair * (2.0 * k_pair - k_pair.T) / (eps_pair - vir_sum[...])
        return jnp.sum(terms.reshape(n_vir // 8, 8, n_vir), axis=0)

    def gram(rows, cols):
        return lax.dot_general(rows, cols, (((1,), (1,)), ((), ())), preferred_element_type=jnp.float32)

    def add_pair(slot_x, orb_x, slot_y, orb_y, k_pair):
        e_vec = energy(k_pair, eps_slot[slot_x, orb_x] + eps_slot[slot_y, orb_y]) * (act_slot[slot_x, orb_x] * act_slot[slot_y, orb_y])
        acc[slot_x, orb_x] += e_vec
        if not (slot_x is slot_y and orb_x == orb_y):
            acc[slot_y, orb_y] += e_vec

    def block_step(slot, carry):
        @pl.when(slot == 2)
        def _():
            for hop, hop_rest, onward, onward_rest in hops:
                hop.wait_recv()
                hop_rest.wait_recv()
                onward.start()
                onward_rest.start()

        @pl.when(slot > 0)
        def _():
            main_copy(slot, me, me).wait_recv()
            rest_copy(slot, me, me).wait_recv()
            tail = rest_in[slot]
            tail = jnp.concatenate([tail[:, part * n_rest:(part + 1) * n_rest] for part in range(fold)], axis=0)
            blocks[slot, :, :, n_main:] = tail.reshape(n_loc, n_vir, n_rest)

        mine = blocks[slot]
        for orb_x in range(n_loc):
            rows = mine[:orb_x + 1].reshape((orb_x + 1) * n_vir, n_aux)
            product = gram(rows, mine[orb_x])
            for orb_y in range(orb_x + 1):
                add_pair(slot, orb_x, slot, orb_y, product[orb_y * n_vir:(orb_y + 1) * n_vir])

        def with_earlier(prior, inner):
            rows = blocks[prior].reshape(n_loc * n_vir, n_aux)
            for orb_x in range(n_loc):
                product = gram(rows, blocks[slot, orb_x])
                for orb_y in range(n_loc):
                    add_pair(slot, orb_x, prior, orb_y, product[orb_y * n_vir:(orb_y + 1) * n_vir])
            return inner

        lax.fori_loop(0, slot, with_earlier, 0)
        return carry

    lax.fori_loop(0, n_dev, block_step, 0)

    e_orb = jnp.sum(jnp.sum(acc[...].reshape(n_dev * n_loc, 8, n_vir), axis=1), axis=1, keepdims=True)
    total = jnp.sum(e_orb, axis=0, keepdims=True)
    copies = []
    for slot, (d_chip, d_core) in enumerate(order):
        result[slot, 0:n_loc, :] = jnp.broadcast_to(e_orb[slot * n_loc:(slot + 1) * n_loc], (n_loc, LANES))
        result[slot, n_loc:n_loc + 1, :] = jnp.broadcast_to(total, (1, LANES))
    for slot in range(1, n_dev):
        main_copy(slot, me, me).wait_send()
        rest_copy(slot, me, me).wait_send()
    for hop, hop_rest, _, _ in hops:
        hop.wait_send()
        hop_rest.wait_send()
    keep = pltpu.make_async_copy(result.at[0], out_ref.at[me], own_sem)
    keep.start()
    for slot, (d_chip, d_core) in enumerate(order):
        if slot > 0:
            copies.append(pltpu.make_async_remote_copy(result.at[slot], out_ref.at[me], res_send_sem.at[slot], res_recv_sem.at[slot], device_id={"occ": device(-d_chip, d_core)}, device_id_type=MESH))
            copies[-1].start()
    keep.wait()
    for copy in copies:
        copy.wait()


def solution(mesh):
    n_dev = mesh.shape["occ"]

    def local_fn(b_own, eps_occ, eps_vir, active):
        b_rows = jnp.transpose(b_own, (0, 2, 3, 1))
        n_frame, n_loc, n_vir, n_aux = b_rows.shape
        n_main = n_aux // LANES * LANES
        fold = LANES // (n_aux - n_main)
        fold_rows = n_loc * n_vir // fold
        vmem, smem, sem = pltpu.VMEM, pltpu.SMEM, pltpu.SemaphoreType.DMA
        out = pl.pallas_call(
            functools.partial(kernel, n_dev),
            out_shape=jax.ShapeDtypeStruct((n_frame, 8, LANES), jnp.float32),
            in_specs=[pl.BlockSpec(memory_space=pl.ANY), pl.BlockSpec(memory_space=smem), pl.BlockSpec(memory_space=smem), pl.BlockSpec(memory_space=vmem)],
            out_specs=pl.BlockSpec(memory_space=vmem),
            scratch_shapes=[
                vmem(b_rows.shape, b_rows.dtype),
                vmem((n_dev, n_loc, n_vir, n_aux), b_rows.dtype),
                vmem((n_dev, fold_rows, LANES), b_rows.dtype),
                vmem((n_dev, fold_rows, LANES), b_rows.dtype),
                vmem((CORES, n_loc, n_vir, n_main), b_rows.dtype),
                vmem((CORES, fold_rows, LANES), b_rows.dtype),
                vmem((n_vir, n_vir), jnp.float32),
                vmem((n_dev, n_loc, 8, n_vir), jnp.float32),
                vmem((n_dev, 8, LANES), jnp.float32),
                smem((n_dev, n_loc), jnp.float32),
                smem((n_dev, n_loc), jnp.float32),
                sem, sem,
                sem((n_dev,)), sem((n_dev,)), sem((n_dev,)), sem((n_dev,)),
                sem((CORES,)), sem((CORES,)), sem((CORES,)), sem((CORES,)),
                sem((n_dev,)), sem((n_dev,)),
            ],
            compiler_params=pltpu.CompilerParams(collective_id=0, has_side_effects=True, vmem_limit_bytes=56 * 2**20),
            cost_estimate=pl.CostEstimate(flops=2 * n_vir * n_vir * n_aux * n_dev * n_loc * (n_dev * n_loc + 1) // 2, bytes_accessed=2 * b_rows.size * 2, transcendentals=0),
            name="pair_energies",
        )(b_rows, eps_occ, active, eps_vir)
        return out[:, 0:n_loc, 0], out[:, n_loc, 0]

    return jax.shard_map(local_fn, mesh=mesh, in_specs=(P("mol", None, "occ", None), P("mol", None), P("mol", None), P("mol", None)), out_specs=(P("mol", "occ"), P("mol")), check_vma=False)
```

time: 872 us -> 199 us (0.23); the launches traced: 858 us -> 199 us
  waiting for transfers between devices: 337 us -> 0 us
  Pallas kernels: 0 us -> 195 us
  matrix products: 152 us -> 0 us
  local copies, waits for them, and re-layouts: 141 us -> 3.05 us
  other arithmetic: 92.6 us -> 0 us
  blocking collectives: 86.3 us -> 0 us
  loops' own time: 32.1 us -> 0 us
  starting transfers between devices: 15.6 us -> 0 us
    ppermute x8 -> x0, waiting for transfers between devices: 337 us -> none  [local_fn(): visiting = lax.ppermute(visiting, 'occ', shift_perm)]
    pallas_call x0 -> x1, Pallas kernels: none -> 195 us  [local_fn(): pl.pallas_call(functools.partial(kernel, n_dev), out_shape=jax.ShapeDtype...]
    dot_general x17 -> x0, matrix products: 152 us -> none  [row_energy(): jnp.einsum('fqa,fqjb->fajb', x_row, y_blk, preferred_element_type=jnp.flo...]
    dot_general x17 -> x0, local copies, waits for them, and re-layouts: 109 us -> none  [row_energy(): jnp.einsum('fqa,fqjb->fajb', x_row, y_blk, preferred_element_type=jnp.flo...]
    reduce_sum x20 -> x0, other arithmetic: 82.9 us -> none  [the longest x17 82.1 us: row_energy(): return jnp.sum(pair_terms, axis=(1, 3))]
    unnamed x1 -> x0, blocking collectives: 59.3 us -> none
    another operation x9 -> x0, loops' own time: 32.1 us -> none  [the longest x8 31.8 us: pair_block(): row_sums = lax.map(row_energy, jnp.arange(x_blk.shape[2]))]
    psum x1 -> x0, blocking collectives: 26.9 us -> none  [local_fn(): energy = lax.psum(jnp.sum(e_pair, axis=1), 'occ')]
  transfers between devices with their start and end apart: 8 -> 0, of which waited for: 4 -> 0; matrix products, arithmetic and copies ran while one was open for 42% -> 0% of each run, Pallas kernels for 0% -> 0%
where the time goes in v1:
time: 199 us
  Pallas kernels  195 us (98%)
  local copies, waits for them, and re-layouts  3.05 us (2%)
    pallas_call x1, Pallas kernels, local_fn(): pl.pallas_call(functools.partial(kernel, n_dev), out_shape=jax.ShapeDtype...  195 us

profile of v1, /device:TPU:21, one launch (start us, length us, event | category | flops | bytes accessed | tf_op | source)
XLA Modules:
  0.0 198.8 jit_solution(6684556264654192735)
XLA Ops:
  0.6 195.2 %pair_energies.1 = f32[16,8,128]{2,1,0:T(8,128)} custom-call(bf16[16,2,160,672]{3,2,1,0:T(8,128)(2,1)} %bitcast.3, f32[16,32]{1,0:T(8,128)} %eps_ref.1, s32[16,32]{1,0:T(8,128)} %act_ref.1, f32[16,160]{1,0:T(8,128)} %vir_ref.1), custom_call_target="tpu_custom_call" | custom-call | flops 18166579200 | bytes 13762560 | tf_op jit(solution)/shard_map/pair_energies/pallas_call | solution.py:177
  195.8 1.6 slice_reduce_fusion
  197.4 0.8 slice.6
  198.2 0.6 copy.7

commit v2 on v1

v2 whole, which is shorter than its diff:
```python
import functools

import jax
import jax.numpy as jnp
from jax import lax
from jax.experimental import pallas as pl
from jax.experimental.pallas import tpu as pltpu
from jax.sharding import PartitionSpec as P

MESH = pl.DeviceIdType.MESH
CORES = 2
LANES = 128


def schedule(n_chip, n_loc):
    half = n_chip // 2
    pairs = [[(dist, core), (-dist, core)] for dist in range(1, half) for core in range(CORES)]
    pairs.insert(0, [(half, core) for core in range(CORES)])
    sources = [(0, 0), (0, 1)] + [disp for pair in pairs for disp in pair]
    slots = [[(source, orb) for orb in range(n_loc)] for source in range(CORES)]
    for first in range(CORES, len(sources), n_loc):
        slots += [[(first + k, orb) for k in range(n_loc)] for orb in range(n_loc)]
    return sources, slots


def kernel(n_dev, b_hbm, eps_ref, act_ref, vir_ref, e_ref, total_ref, local, blocks, rest_out, rest_in, vir_sum, product, acc, result, returned, eps_slot, act_slot, load_sem, own_sem, send_sem, recv_sem, rest_send_sem, rest_recv_sem, res_send_sem, res_recv_sem):
    n_chip = n_dev // CORES
    n_slot, n_loc, n_vir, n_aux = blocks.shape
    sources, slots = schedule(n_chip, n_loc)
    n_main = n_aux // LANES * LANES
    n_rest = n_aux - n_main
    fold = LANES // n_rest
    fold_rows = n_loc * n_vir // fold
    me = lax.axis_index("occ")
    chip, core = me // CORES, me % CORES
    main = pl.ds(0, n_main)

    def device(d_chip, d_core):
        return (chip + d_chip + n_chip) % n_chip * CORES + (core + d_core) % CORES

    targets = [device(d_chip, d_core) for d_chip, d_core in sources]
    owners = [device(-d_chip, d_core) for d_chip, d_core in sources]

    barrier = pltpu.get_barrier_semaphore()
    for step in range(1, n_dev):
        pl.semaphore_signal(barrier, inc=1, device_id={"occ": (me + step) % n_dev}, device_id_type=MESH)
    load = pltpu.make_async_copy(b_hbm, local, load_sem)
    load.start()
    own = pltpu.make_async_copy(b_hbm.at[me], blocks.at[0], own_sem)
    own.start()

    for slot, members in enumerate(slots):
        for k, (source, orb) in enumerate(members):
            eps_slot[slot, k] = eps_ref[me, owners[source] * n_loc + orb]
            act_slot[slot, k] = act_ref[me, owners[source] * n_loc + orb].astype(jnp.float32)
    vir_row = jnp.broadcast_to(vir_ref[pl.ds(me, 1), :], (n_vir, n_vir))
    vir_sum[...] = vir_row + vir_row.T
    acc[...] = jnp.zeros_like(acc)
    load.wait()

    def pack(frame, carry):
        tail = local[frame, :, :, n_main:].reshape(n_loc * n_vir, n_rest)
        rest_out[frame] = jnp.concatenate([tail[part * fold_rows:(part + 1) * fold_rows] for part in range(fold)], axis=1)
        return carry

    lax.fori_loop(0, n_dev, pack, 0)
    pl.semaphore_wait(barrier, n_dev - 1)

    def main_copy(slot, k, orb, target):
        return pltpu.make_async_remote_copy(b_hbm.at[target, orb, :, main], blocks.at[slot, k, :, main], send_sem.at[slot, k], recv_sem.at[slot, k], device_id={"occ": target}, device_id_type=MESH)

    def rest_copy(source, target):
        return pltpu.make_async_remote_copy(rest_out.at[target], rest_in.at[source], rest_send_sem.at[source], rest_recv_sem.at[source], device_id={"occ": target}, device_id_type=MESH)

    for slot, members in enumerate(slots):
        for k, (source, orb) in enumerate(members):
            if source > 0:
                if orb == 0:
                    rest_copy(source, targets[source]).start()
                main_copy(slot, k, orb, targets[source]).start()
    own.wait()

    def multiply(slot, prior):
        rows = blocks[prior].reshape(n_loc * n_vir, n_aux)
        for x in range(n_loc):
            product[x] = lax.dot_general(rows, blocks[slot, x], (((1,), (1,)), ((), ())), preferred_element_type=jnp.float32)

    def add_energies(slot, prior):
        cross = jnp.where(slot == prior, 0.0, 1.0)
        columns = [None] * n_loc
        for x in range(n_loc):
            row = None
            for y in range(n_loc):
                k_pair = product[x, y * n_vir:(y + 1) * n_vir]
                terms = k_pair * (2.0 * k_pair - k_pair.T) / ((eps_slot[slot, x] + eps_slot[prior, y]) - vir_sum[...])
                e_vec = jnp.sum(terms.reshape(n_vir // 8, 8, n_vir), axis=0) * (act_slot[slot, x] * act_slot[prior, y])
                row = e_vec if row is None else row + e_vec
                columns[y] = e_vec if columns[y] is None else columns[y] + e_vec
            acc[slot, x] += row
        for y in range(n_loc):
            acc[prior, y] += columns[y] * cross

    def arrive(slot):
        def unpack(slot, k, source, orb):
            part_rows = n_vir // fold_rows if n_vir >= fold_rows else 1
            tail = rest_in[source]
            parts = [tail[:, part * n_rest:(part + 1) * n_rest] for part in range(orb * part_rows, (orb + 1) * part_rows)]
            blocks[slot, k, :, n_main:] = jnp.concatenate(parts, axis=0)

        for index, members in enumerate(slots):
            if index > 0:
                @pl.when(slot == index)
                def _(index=index, members=members):
                    for k, (source, orb) in enumerate(members):
                        if orb == 0:
                            rest_copy(source, me).wait_recv()
                        main_copy(index, k, orb, me).wait_recv()
                        unpack(index, k, source, orb)

    def slot_step(slot, carry):
        arrive(slot)

        def prior_step(prior, last):
            add_energies(*last)
            multiply(slot, prior)
            return slot, prior

        return lax.fori_loop(0, slot + 1, prior_step, carry)

    multiply(0, 0)
    last = lax.fori_loop(1, n_slot, slot_step, (jnp.int32(0), jnp.int32(0)))
    add_energies(*last)

    e_orb = jnp.sum(jnp.sum(acc[...].reshape(n_slot * n_loc, 8, n_vir), axis=1), axis=1, keepdims=True)
    total = jnp.sum(e_orb, axis=0, keepdims=True)
    where_is = {member: slot * n_loc + k for slot, members in enumerate(slots) for k, member in enumerate(members)}
    lane = lax.broadcasted_iota(jnp.int32, (8, LANES), 1)
    for source in range(n_dev):
        tile = jnp.broadcast_to(total, (8, LANES))
        for orb in range(n_loc):
            at = where_is[source, orb]
            tile = jnp.where(lane == orb, jnp.broadcast_to(e_orb[at:at + 1], (8, LANES)), tile)
        result[source] = tile
    for slot, members in enumerate(slots):
        for k, (source, orb) in enumerate(members):
            if source > 0:
                main_copy(slot, k, orb, me).wait_send()
                if orb == 0:
                    rest_copy(source, me).wait_send()
    copies = []
    for source in range(1, n_dev):
        copies.append(pltpu.make_async_remote_copy(result.at[source], returned.at[me], res_send_sem.at[source], res_recv_sem.at[source], device_id={"occ": owners[source]}, device_id_type=MESH))
        copies[-1].start()
    returned[me] = result[0]
    for copy in copies:
        copy.wait()
    rows = returned[:, 0, :]
    e_ref[...] = rows[:, 0:n_loc]
    total_ref[...] = rows.T[n_loc:n_loc + 1, :]


def solution(mesh):
    n_dev = mesh.shape["occ"]

    def local_fn(b_own, eps_occ, eps_vir, active):
        b_rows = jnp.transpose(b_own, (0, 2, 3, 1))
        n_frame, n_loc, n_vir, n_aux = b_rows.shape
        fold = LANES // (n_aux % LANES)
        fold_rows = n_loc * n_vir // fold
        n_orb = n_dev * n_loc
        vmem, smem, sem = pltpu.VMEM, pltpu.SMEM, pltpu.SemaphoreType.DMA
        e_pair, energy = pl.pallas_call(
            functools.partial(kernel, n_dev),
            out_shape=(jax.ShapeDtypeStruct((n_frame, n_loc), jnp.float32), jax.ShapeDtypeStruct((1, n_frame), jnp.float32)),
            in_specs=[pl.BlockSpec(memory_space=pl.ANY), pl.BlockSpec(memory_space=smem), pl.BlockSpec(memory_space=smem), pl.BlockSpec(memory_space=vmem)],
            out_specs=(pl.BlockSpec(memory_space=vmem), pl.BlockSpec(memory_space=vmem)),
            scratch_shapes=[
                vmem(b_rows.shape, b_rows.dtype),
                vmem((n_dev, n_loc, n_vir, n_aux), b_rows.dtype),
                vmem((n_dev, fold_rows, LANES), b_rows.dtype),
                vmem((n_dev, fold_rows, LANES), b_rows.dtype),
                vmem((n_vir, n_vir), jnp.float32),
                vmem((n_loc, n_loc * n_vir, n_vir), jnp.float32),
                vmem((n_dev, n_loc, 8, n_vir), jnp.float32),
                vmem((n_dev, 8, LANES), jnp.float32),
                vmem((n_dev, 8, LANES), jnp.float32),
                smem((n_dev, n_loc), jnp.float32),
                smem((n_dev, n_loc), jnp.float32),
                sem, sem,
                sem((n_dev, n_loc)), sem((n_dev, n_loc)), sem((n_dev,)), sem((n_dev,)),
                sem((n_dev,)), sem((n_dev,)),
            ],
            compiler_params=pltpu.CompilerParams(collective_id=0, has_side_effects=True, vmem_limit_bytes=56 * 2**20),
            cost_estimate=pl.CostEstimate(flops=n_vir * n_vir * n_aux * n_orb * (n_orb + 1), bytes_accessed=2 * b_rows.size * 2, transcendentals=0),
            name="pair_energies",
        )(b_rows, eps_occ, active, eps_vir)
        return e_pair, energy[0]

    return jax.shard_map(local_fn, mesh=mesh, in_specs=(P("mol", None, "occ", None), P("mol", None), P("mol", None), P("mol", None)), out_specs=(P("mol", "occ"), P("mol")), check_vma=False)
```

time: 199 us -> 180 us (0.905)
  Pallas kernels: 195 us -> 177 us
    pallas_call x1, Pallas kernels: 195 us -> 177 us  [local_fn(): pl.pallas_call(functools.partial(kernel, n_dev), out_shape=(jax.ShapeDtyp...]
    slice x3 -> x0, local copies, waits for them, and re-layouts: 3.05 us -> none  [local_fn(): return (out[:, 0:n_loc, 0], out[:, n_loc, 0])]
    unnamed x0 -> x2, local copies, waits for them, and re-layouts: none -> 2.47 us
where the time goes in v2:
time: 180 us
  Pallas kernels  177 us (98%)
  local copies, waits for them, and re-layouts  2.47 us (1%)
    pallas_call x1, Pallas kernels, local_fn(): pl.pallas_call(functools.partial(kernel, n_dev), out_shape=(jax.ShapeDtyp...  177 us

profile of v2, /device:TPU:21, one launch (start us, length us, event | category | flops | bytes accessed | tf_op | source)
XLA Modules:
  0.0 180.2 jit_solution(6783417300773263919)
XLA Ops:
  0.6 177.1 %pair_energies.1 = (f32[16,2]{1,0:T(8,128)}, f32[1,16]{1,0:T(1,128)}) custom-call(bf16[16,2,160,672]{3,2,1,0:T(8,128)(2,1)} %bitcast.2, f32[16,32]{1,0:T(8,128)} %eps_ref.1, s32[16,32]{1,0:T(8,128)} %act_ref.1, f32[16,160]{1,0:T(8,128)} %vir_ref.1), custom_call_target="tpu_custom_call" | custom-call | flops 18166579200 | bytes 13762560 | tf_op jit(solution)/shard_map/pair_energies/pallas_call | solution.py:172
  177.7 1.3 copy.6
  179.0 1.1 copy.8

commit v3 on v2

--- a/solution.py
+++ b/solution.py
@@ -10,6 +10,7 @@
 MESH = pl.DeviceIdType.MESH
 CORES = 2
 LANES = 128
+GROUP = 4
 
 
 def schedule(n_chip, n_loc):
@@ -23,7 +24,7 @@
     return sources, slots
 
 
-def kernel(n_dev, b_hbm, eps_ref, act_ref, vir_ref, e_ref, total_ref, local, blocks, rest_out, rest_in, vir_sum, product, acc, result, returned, eps_slot, act_slot, load_sem, own_sem, send_sem, recv_sem, rest_send_sem, rest_recv_sem, res_send_sem, res_recv_sem):
+def kernel(n_dev, b_hbm, eps_hbm, act_hbm, vir_hbm, out_ref, eps_ref, act_ref, vir_ref, local, blocks, rest_out, rest_in, vir_sum, product, acc, result, returned, eps_slot, act_slot, small_sem, load_sem, own_sem, send_sem, recv_sem, rest_send_sem, rest_recv_sem, res_send_sem, res_recv_sem):
     n_chip = n_dev // CORES
     n_slot, n_loc, n_vir, n_aux = blocks.shape
     sources, slots = schedule(n_chip, n_loc)
@@ -44,10 +45,16 @@
     barrier = pltpu.get_barrier_semaphore()
     for step in range(1, n_dev):
         pl.semaphore_signal(barrier, inc=1, device_id={"occ": (me + step) % n_dev}, device_id_type=MESH)
+    small = [pltpu.make_async_copy(source, target, small_sem.at[k]) for k, (source, target) in enumerate(((eps_hbm, eps_ref), (act_hbm, act_ref), (vir_hbm, vir_ref)))]
+    for copy in small:
+        copy.start()
     load = pltpu.make_async_copy(b_hbm, local, load_sem)
     load.start()
     own = pltpu.make_async_copy(b_hbm.at[me], blocks.at[0], own_sem)
     own.start()
+    acc[...] = jnp.zeros_like(acc)
+    for copy in small:
+        copy.wait()
 
     for slot, members in enumerate(slots):
         for k, (source, orb) in enumerate(members):
@@ -55,7 +62,6 @@
             act_slot[slot, k] = act_ref[me, owners[source] * n_loc + orb].astype(jnp.float32)
     vir_row = jnp.broadcast_to(vir_ref[pl.ds(me, 1), :], (n_vir, n_vir))
     vir_sum[...] = vir_row + vir_row.T
-    acc[...] = jnp.zeros_like(acc)
     load.wait()
 
     def pack(frame, carry):
@@ -80,55 +86,72 @@
                 main_copy(slot, k, orb, targets[source]).start()
     own.wait()
 
-    def multiply(slot, prior):
-        rows = blocks[prior].reshape(n_loc * n_vir, n_aux)
+    def multiply(slot, first):
+        rows = blocks[pl.ds(first, GROUP)].reshape(GROUP * n_loc * n_vir, n_aux)
         for x in range(n_loc):
             product[x] = lax.dot_general(rows, blocks[slot, x], (((1,), (1,)), ((), ())), preferred_element_type=jnp.float32)
 
-    def add_energies(slot, prior):
-        cross = jnp.where(slot == prior, 0.0, 1.0)
-        columns = [None] * n_loc
+    def fold_rows_of(terms):
+        return jnp.sum(terms.reshape(terms.shape[0] // 8, 8, terms.shape[1]), axis=0)
+
+    def pair_terms(k_ref, eps_pair):
+        low, high = pl.ds(0, LANES), pl.ds(LANES, n_vir - LANES)
+        def same(part):
+            k_part = k_ref[part, part]
+            return fold_rows_of(k_part * (2.0 * k_part - k_part.T) / (eps_pair - vir_sum[part, part]))
+        k_ab, k_ba = k_ref[high, low], k_ref[low, high].T
+        mixed = (2.0 * (k_ab * (k_ab - k_ba) + k_ba * k_ba)) / (eps_pair - vir_sum[high, low])
+        return jnp.concatenate([same(low) + fold_rows_of(mixed), same(high)], axis=1)
+
+    def add_energies(slot, first, fresh):
+        row = [jnp.zeros(acc.shape[2:], jnp.float32)] * n_loc
+        for g in range(GROUP):
+            prior = first + g
+            counts = jnp.where((prior >= fresh) & (prior <= slot), 1.0, 0.0)
+            cross = jnp.where(prior == slot, 0.0, 1.0)
+            for y in range(n_loc):
+                column = None
+                for x in range(n_loc):
+                    at = (g * n_loc + y) * n_vir
+                    e_vec = pair_terms(product.at[x, pl.ds(at, n_vir)], eps_slot[slot, x] + eps_slot[prior, y]) * (act_slot[slot, x] * act_slot[prior, y] * counts)
+                    row[x] = row[x] + e_vec
+                    column = e_vec if column is None else column + e_vec
+                acc[prior, y] += column * cross
         for x in range(n_loc):
-            row = None
-            for y in range(n_loc):
-                k_pair = product[x, y * n_vir:(y + 1) * n_vir]
-                terms = k_pair * (2.0 * k_pair - k_pair.T) / ((eps_slot[slot, x] + eps_slot[prior, y]) - vir_sum[...])
-                e_vec = jnp.sum(terms.reshape(n_vir // 8, 8, n_vir), axis=0) * (act_slot[slot, x] * act_slot[prior, y])
-                row = e_vec if row is None else row + e_vec
-                columns[y] = e_vec if columns[y] is None else columns[y] + e_vec
-            acc[slot, x] += row
-        for y in range(n_loc):
-            acc[prior, y] += columns[y] * cross
-
-    def arrive(slot):
+            acc[slot, x] += row[x]
+
+    def arrive(slot, indices):
         def unpack(slot, k, source, orb):
             part_rows = n_vir // fold_rows if n_vir >= fold_rows else 1
             tail = rest_in[source]
             parts = [tail[:, part * n_rest:(part + 1) * n_rest] for part in range(orb * part_rows, (orb + 1) * part_rows)]
             blocks[slot, k, :, n_main:] = jnp.concatenate(parts, axis=0)
 
-        for index, members in enumerate(slots):
-            if index > 0:
-                @pl.when(slot == index)
-                def _(index=index, members=members):
-                    for k, (source, orb) in enumerate(members):
-                        if orb == 0:
-                            rest_copy(source, me).wait_recv()
-                        main_copy(index, k, orb, me).wait_recv()
-                        unpack(index, k, source, orb)
+        for index in indices:
+            @pl.when(slot == index)
+            def _(index=index):
+                for k, (source, orb) in enumerate(slots[index]):
+                    if orb == 0:
+                        rest_copy(source, me).wait_recv()
+                    main_copy(index, k, orb, me).wait_recv()
+                    unpack(index, k, source, orb)
 
     def slot_step(slot, carry):
-        arrive(slot)
-
-        def prior_step(prior, last):
+        arrive(slot, range(GROUP, n_slot))
+
+        def group_step(step, last):
+            fresh = step * GROUP
+            first = jnp.maximum(jnp.minimum(fresh, slot + 1 - GROUP), 0)
             add_energies(*last)
-            multiply(slot, prior)
-            return slot, prior
-
-        return lax.fori_loop(0, slot + 1, prior_step, carry)
-
+            multiply(slot, first)
+            return slot, first, fresh
+
+        return lax.fori_loop(0, slot // GROUP + 1, group_step, carry)
+
+    for index in range(1, GROUP):
+        arrive(index, [index])
     multiply(0, 0)
-    last = lax.fori_loop(1, n_slot, slot_step, (jnp.int32(0), jnp.int32(0)))
+    last = lax.fori_loop(1, n_slot, slot_step, (jnp.int32(0), jnp.int32(0), jnp.int32(0)))
     add_energies(*last)
 
     e_orb = jnp.sum(jnp.sum(acc[...].reshape(n_slot * n_loc, 8, n_vir), axis=1), axis=1, keepdims=True)
@@ -149,14 +172,17 @@
                     rest_copy(source, me).wait_send()
     copies = []
     for source in range(1, n_dev):
-        copies.append(pltpu.make_async_remote_copy(result.at[source], returned.at[me], res_send_sem.at[source], res_recv_sem.at[source], device_id={"occ": owners[source]}, device_id_type=MESH))
+        copies.append(pltpu.make_async_remote_copy(result.at[source, pl.ds(0, 1)], returned.at[me, pl.ds(0, 1)], res_send_sem.at[source], res_recv_sem.at[source], device_id={"occ": owners[source]}, device_id_type=MESH))
         copies[-1].start()
     returned[me] = result[0]
     for copy in copies:
         copy.wait()
-    rows = returned[:, 0, :]
-    e_ref[...] = rows[:, 0:n_loc]
-    total_ref[...] = rows.T[n_loc:n_loc + 1, :]
+    out_ref[...] = returned[:, 0, :].T[0:8]
+
+
+def finish(rows_ref, e_ref, total_ref):
+    e_ref[...] = rows_ref[0:e_ref.shape[0], :]
+    total_ref[...] = rows_ref[e_ref.shape[0]:e_ref.shape[0] + 1, :]
 
 
 def solution(mesh):
@@ -169,24 +195,27 @@
         fold_rows = n_loc * n_vir // fold
         n_orb = n_dev * n_loc
         vmem, smem, sem = pltpu.VMEM, pltpu.SMEM, pltpu.SemaphoreType.DMA
-        e_pair, energy = pl.pallas_call(
+        rows = pl.pallas_call(
             functools.partial(kernel, n_dev),
-            out_shape=(jax.ShapeDtypeStruct((n_frame, n_loc), jnp.float32), jax.ShapeDtypeStruct((1, n_frame), jnp.float32)),
-            in_specs=[pl.BlockSpec(memory_space=pl.ANY), pl.BlockSpec(memory_space=smem), pl.BlockSpec(memory_space=smem), pl.BlockSpec(memory_space=vmem)],
-            out_specs=(pl.BlockSpec(memory_space=vmem), pl.BlockSpec(memory_space=vmem)),
+            out_shape=jax.ShapeDtypeStruct((8, n_frame), jnp.float32),
+            in_specs=[pl.BlockSpec(memory_space=pl.ANY)] * 4,
+            out_specs=pl.BlockSpec(memory_space=vmem),
             scratch_shapes=[
+                smem(eps_occ.shape, eps_occ.dtype),
+                smem(active.shape, active.dtype),
+                vmem(eps_vir.shape, eps_vir.dtype),
                 vmem(b_rows.shape, b_rows.dtype),
                 vmem((n_dev, n_loc, n_vir, n_aux), b_rows.dtype),
                 vmem((n_dev, fold_rows, LANES), b_rows.dtype),
                 vmem((n_dev, fold_rows, LANES), b_rows.dtype),
                 vmem((n_vir, n_vir), jnp.float32),
-                vmem((n_loc, n_loc * n_vir, n_vir), jnp.float32),
+                vmem((n_loc, GROUP * n_loc * n_vir, n_vir), jnp.float32),
                 vmem((n_dev, n_loc, 8, n_vir), jnp.float32),
                 vmem((n_dev, 8, LANES), jnp.float32),
                 vmem((n_dev, 8, LANES), jnp.float32),
                 smem((n_dev, n_loc), jnp.float32),
                 smem((n_dev, n_loc), jnp.float32),
-                sem, sem,
+                sem((3,)), sem, sem,
                 sem((n_dev, n_loc)), sem((n_dev, n_loc)), sem((n_dev,)), sem((n_dev,)),
                 sem((n_dev,)), sem((n_dev,)),
             ],
@@ -194,6 +223,13 @@
             cost_estimate=pl.CostEstimate(flops=n_vir * n_vir * n_aux * n_orb * (n_orb + 1), bytes_accessed=2 * b_rows.size * 2, transcendentals=0),
             name="pair_energies",
         )(b_rows, eps_occ, active, eps_vir)
-        return e_pair, energy[0]
+        e_pair, energy = pl.pallas_call(
+            finish,
+            out_shape=(jax.ShapeDtypeStruct((n_loc, n_frame), jnp.float32), jax.ShapeDtypeStruct((1, n_frame), jnp.float32)),
+            in_specs=[pl.BlockSpec(memory_space=vmem)],
+            out_specs=(pl.BlockSpec(memory_space=vmem), pl.BlockSpec(memory_space=vmem)),
+            name="finish",
+        )(rows)
+        return e_pair.T, energy[0]
 
     return jax.shard_map(local_fn, mesh=mesh, in_specs=(P("mol", None, "occ", None), P("mol", None), P("mol", None), P("mol", None)), out_specs=(P("mol", "occ"), P("mol")), check_vma=False)

time: 180 us -> 176 us (0.978)
  local copies, waits for them, and re-layouts: 2.47 us -> 0 us
  Pallas kernels: 177 us -> 175 us
    unnamed x2 -> x0, local copies, waits for them, and re-layouts: 2.47 us -> none
    pallas_call x1 -> x2, Pallas kernels: 177 us -> 175 us  [the longest x1 174 us: local_fn(): pl.pallas_call(functools.partial(kernel, n_dev), out_shape=jax.ShapeDtype...]
where the time goes in v3:
time: 176 us
  Pallas kernels  175 us (99%)
    pallas_call x1, Pallas kernels, local_fn(): pl.pallas_call(functools.partial(kernel, n_dev), out_shape=jax.ShapeDtype...  174 us

profile of v3, /device:TPU:21, one launch (start us, length us, event | category | flops | bytes accessed | tf_op | source)
XLA Modules:
  0.0 175.7 jit_solution(6321017894410146075)
XLA Ops:
  0.6 173.8 %pair_energies.1.rows_ref = f32[8,16]{1,0:T(8,128)} custom-call(bf16[16,2,160,672]{3,2,1,0:T(8,128)(2,1)} %bitcast.3, f32[16,32]{1,0:T(8,128)} %eps_hbm.1, s32[16,32]{1,0:T(8,128)} %act_hbm.1, f32[16,160]{1,0:T(8,128)} %vir_hbm.1), custom_call_target="tpu_custom_call" | custom-call | flops 18166579200 | bytes 13762560 | tf_op jit(solution)/shard_map/pair_energies/pallas_call | solution.py:198
  174.5 1.2 finish.1

commit v4 on v3

--- a/solution.py
+++ b/solution.py
@@ -10,6 +10,7 @@
 MESH = pl.DeviceIdType.MESH
 CORES = 2
 LANES = 128
+SPLIT = 256
 GROUP = 4
 
 
@@ -24,7 +25,7 @@
     return sources, slots
 
 
-def kernel(n_dev, b_hbm, eps_hbm, act_hbm, vir_hbm, out_ref, eps_ref, act_ref, vir_ref, local, blocks, rest_out, rest_in, vir_sum, product, acc, result, returned, eps_slot, act_slot, small_sem, load_sem, own_sem, send_sem, recv_sem, rest_send_sem, rest_recv_sem, res_send_sem, res_recv_sem):
+def kernel(n_dev, b_hbm, eps_hbm, act_hbm, vir_hbm, out_ref, eps_ref, act_ref, vir_ref, local, blocks, rest_out, rest_in, vir_sum, product, partial, acc, result, returned, eps_slot, act_slot, small_sem, load_sem, own_sem, send_sem, recv_sem, late_send_sem, late_recv_sem, rest_send_sem, rest_recv_sem, res_send_sem, res_recv_sem):
     n_chip = n_dev // CORES
     n_slot, n_loc, n_vir, n_aux = blocks.shape
     sources, slots = schedule(n_chip, n_loc)
@@ -34,7 +35,7 @@
     fold_rows = n_loc * n_vir // fold
     me = lax.axis_index("occ")
     chip, core = me // CORES, me % CORES
-    main = pl.ds(0, n_main)
+    main, head = pl.ds(0, n_main), pl.ds(0, SPLIT)
 
     def device(d_chip, d_core):
         return (chip + d_chip + n_chip) % n_chip * CORES + (core + d_core) % CORES
@@ -45,51 +46,66 @@
     barrier = pltpu.get_barrier_semaphore()
     for step in range(1, n_dev):
         pl.semaphore_signal(barrier, inc=1, device_id={"occ": (me + step) % n_dev}, device_id_type=MESH)
+    load = pltpu.make_async_copy(b_hbm.at[:, :, :, pl.ds(n_main, n_rest)], local, load_sem)
+    load.start()
+    own = pltpu.make_async_copy(b_hbm.at[me], blocks.at[0], own_sem)
+    own.start()
     small = [pltpu.make_async_copy(source, target, small_sem.at[k]) for k, (source, target) in enumerate(((eps_hbm, eps_ref), (act_hbm, act_ref), (vir_hbm, vir_ref)))]
     for copy in small:
         copy.start()
-    load = pltpu.make_async_copy(b_hbm, local, load_sem)
-    load.start()
-    own = pltpu.make_async_copy(b_hbm.at[me], blocks.at[0], own_sem)
-    own.start()
+
+    def lanes_copy(slot, k, orb, target, lanes, sends, recvs):
+        return pltpu.make_async_remote_copy(b_hbm.at[target, orb, :, lanes], blocks.at[slot, k, :, lanes], sends, recvs, device_id={"occ": target}, device_id_type=MESH)
+
+    def main_copy(slot, k, orb, target):
+        lanes = head if slot == n_slot - 1 else main
+        return lanes_copy(slot, k, orb, target, lanes, send_sem.at[slot, k], recv_sem.at[slot, k])
+
+    def late_copy(k, orb, target):
+        return lanes_copy(n_slot - 1, k, orb, target, pl.ds(SPLIT, n_main - SPLIT), late_send_sem.at[k], late_recv_sem.at[k])
+
+    def rest_copy(source, target):
+        return pltpu.make_async_remote_copy(rest_out.at[target], rest_in.at[source], rest_send_sem.at[source], rest_recv_sem.at[source], device_id={"occ": target}, device_id_type=MESH)
+
+    def send_slots(indices):
+        for slot in indices:
+            for k, (source, orb) in enumerate(slots[slot]):
+                main_copy(slot, k, orb, targets[source]).start()
+
+    def pack(frame, carry):
+        tail = local[frame].reshape(n_loc * n_vir, n_rest)
+        rest_out[frame] = jnp.concatenate([tail[part * fold_rows:(part + 1) * fold_rows] for part in range(fold)], axis=1)
+        return carry
+
+    load.wait()
+    lax.fori_loop(0, n_dev, pack, 0)
+    pl.semaphore_wait(barrier, n_dev - 1)
+    for source in range(1, n_dev):
+        rest_copy(source, targets[source]).start()
+    send_slots(range(1, n_slot))
+    for k, (source, orb) in enumerate(slots[-1]):
+        late_copy(k, orb, targets[source]).start()
+
     acc[...] = jnp.zeros_like(acc)
+    result[...] = jnp.zeros_like(result)
     for copy in small:
         copy.wait()
-
     for slot, members in enumerate(slots):
         for k, (source, orb) in enumerate(members):
             eps_slot[slot, k] = eps_ref[me, owners[source] * n_loc + orb]
             act_slot[slot, k] = act_ref[me, owners[source] * n_loc + orb].astype(jnp.float32)
     vir_row = jnp.broadcast_to(vir_ref[pl.ds(me, 1), :], (n_vir, n_vir))
     vir_sum[...] = vir_row + vir_row.T
-    load.wait()
-
-    def pack(frame, carry):
-        tail = local[frame, :, :, n_main:].reshape(n_loc * n_vir, n_rest)
-        rest_out[frame] = jnp.concatenate([tail[part * fold_rows:(part + 1) * fold_rows] for part in range(fold)], axis=1)
-        return carry
-
-    lax.fori_loop(0, n_dev, pack, 0)
-    pl.semaphore_wait(barrier, n_dev - 1)
-
-    def main_copy(slot, k, orb, target):
-        return pltpu.make_async_remote_copy(b_hbm.at[target, orb, :, main], blocks.at[slot, k, :, main], send_sem.at[slot, k], recv_sem.at[slot, k], device_id={"occ": target}, device_id_type=MESH)
-
-    def rest_copy(source, target):
-        return pltpu.make_async_remote_copy(rest_out.at[target], rest_in.at[source], rest_send_sem.at[source], rest_recv_sem.at[source], device_id={"occ": target}, device_id_type=MESH)
-
-    for slot, members in enumerate(slots):
-        for k, (source, orb) in enumerate(members):
-            if source > 0:
-                if orb == 0:
-                    rest_copy(source, targets[source]).start()
-                main_copy(slot, k, orb, targets[source]).start()
     own.wait()
 
+    def gram(slot, x, first, lanes):
+        rows = blocks[pl.ds(first, GROUP), :, :, lanes]
+        cols = blocks[slot, x, :, lanes]
+        return lax.dot_general(rows.reshape(GROUP * n_loc * n_vir, cols.shape[1]), cols, (((1,), (1,)), ((), ())), preferred_element_type=jnp.float32)
+
     def multiply(slot, first):
-        rows = blocks[pl.ds(first, GROUP)].reshape(GROUP * n_loc * n_vir, n_aux)
-        for x in range(n_loc):
-            product[x] = lax.dot_general(rows, blocks[slot, x], (((1,), (1,)), ((), ())), preferred_element_type=jnp.float32)
+        for x in range(n_loc):
+            product[x] = gram(slot, x, first, slice(None))
 
     def fold_rows_of(terms):
         return jnp.sum(terms.reshape(terms.shape[0] // 8, 8, terms.shape[1]), axis=0)
@@ -120,13 +136,13 @@
         for x in range(n_loc):
             acc[slot, x] += row[x]
 
+    def unpack(slot, k, source, orb):
+        part_rows = n_vir // fold_rows if n_vir >= fold_rows else 1
+        tail = rest_in[source]
+        parts = [tail[:, part * n_rest:(part + 1) * n_rest] for part in range(orb * part_rows, (orb + 1) * part_rows)]
+        blocks[slot, k, :, n_main:] = jnp.concatenate(parts, axis=0)
+
     def arrive(slot, indices):
-        def unpack(slot, k, source, orb):
-            part_rows = n_vir // fold_rows if n_vir >= fold_rows else 1
-            tail = rest_in[source]
-            parts = [tail[:, part * n_rest:(part + 1) * n_rest] for part in range(orb * part_rows, (orb + 1) * part_rows)]
-            blocks[slot, k, :, n_main:] = jnp.concatenate(parts, axis=0)
-
         for index in indices:
             @pl.when(slot == index)
             def _(index=index):
@@ -137,7 +153,7 @@
                     unpack(index, k, source, orb)
 
     def slot_step(slot, carry):
-        arrive(slot, range(GROUP, n_slot))
+        arrive(slot, range(GROUP, n_slot - 1))
 
         def group_step(step, last):
             fresh = step * GROUP
@@ -151,8 +167,35 @@
     for index in range(1, GROUP):
         arrive(index, [index])
     multiply(0, 0)
-    last = lax.fori_loop(1, n_slot, slot_step, (jnp.int32(0), jnp.int32(0), jnp.int32(0)))
+    last = lax.fori_loop(1, n_slot - 1, slot_step, (jnp.int32(0), jnp.int32(0), jnp.int32(0)))
     add_energies(*last)
+
+    final = n_slot - 1
+    for k, (source, orb) in enumerate(slots[final]):
+        main_copy(final, k, orb, me).wait_recv()
+
+    def head_step(step, carry):
+        for x in range(n_loc):
+            partial[step, x] = gram(final, x, step * GROUP, slice(0, SPLIT))
+        return carry
+
+    lax.fori_loop(0, n_slot // GROUP, head_step, 0)
+    for k, (source, orb) in enumerate(slots[final]):
+        late_copy(k, orb, me).wait_recv()
+        unpack(final, k, source, orb)
+
+    def finish_product(step):
+        for x in range(n_loc):
+            product[x] = partial[step, x] + gram(final, x, step * GROUP, slice(SPLIT, n_aux))
+
+    def tail_step(step, carry):
+        add_energies(final, (step - 1) * GROUP, (step - 1) * GROUP)
+        finish_product(step)
+        return carry
+
+    finish_product(0)
+    lax.fori_loop(1, n_slot // GROUP, tail_step, 0)
+    add_energies(final, n_slot - GROUP, n_slot - GROUP)
 
     e_orb = jnp.sum(jnp.sum(acc[...].reshape(n_slot * n_loc, 8, n_vir), axis=1), axis=1, keepdims=True)
     total = jnp.sum(e_orb, axis=0, keepdims=True)
@@ -168,6 +211,8 @@
         for k, (source, orb) in enumerate(members):
             if source > 0:
                 main_copy(slot, k, orb, me).wait_send()
+                if slot == final:
+                    late_copy(k, orb, me).wait_send()
                 if orb == 0:
                     rest_copy(source, me).wait_send()
     copies = []
@@ -204,19 +249,20 @@
                 smem(eps_occ.shape, eps_occ.dtype),
                 smem(active.shape, active.dtype),
                 vmem(eps_vir.shape, eps_vir.dtype),
-                vmem(b_rows.shape, b_rows.dtype),
+                vmem((n_frame, n_loc, n_vir, n_aux % LANES), b_rows.dtype),
                 vmem((n_dev, n_loc, n_vir, n_aux), b_rows.dtype),
                 vmem((n_dev, fold_rows, LANES), b_rows.dtype),
                 vmem((n_dev, fold_rows, LANES), b_rows.dtype),
                 vmem((n_vir, n_vir), jnp.float32),
                 vmem((n_loc, GROUP * n_loc * n_vir, n_vir), jnp.float32),
+                vmem((n_dev // GROUP, n_loc, GROUP * n_loc * n_vir, n_vir), jnp.float32),
                 vmem((n_dev, n_loc, 8, n_vir), jnp.float32),
                 vmem((n_dev, 8, LANES), jnp.float32),
                 vmem((n_dev, 8, LANES), jnp.float32),
                 smem((n_dev, n_loc), jnp.float32),
                 smem((n_dev, n_loc), jnp.float32),
                 sem((3,)), sem, sem,
-                sem((n_dev, n_loc)), sem((n_dev, n_loc)), sem((n_dev,)), sem((n_dev,)),
+                sem((n_dev, n_loc)), sem((n_dev, n_loc)), sem((n_loc,)), sem((n_loc,)), sem((n_dev,)), sem((n_dev,)),
                 sem((n_dev,)), sem((n_dev,)),
             ],
             compiler_params=pltpu.CompilerParams(collective_id=0, has_side_effects=True, vmem_limit_bytes=56 * 2**20),

time: 176 us -> 173 us (0.983)
  Pallas kernels: 175 us -> 172 us
    pallas_call x1, Pallas kernels: 174 us -> 171 us  [local_fn(): pl.pallas_call(functools.partial(kernel, n_dev), out_shape=jax.ShapeDtype...]
where the time goes in v4:
time: 173 us; the launch traced here: 172 us
  Pallas kernels  172 us (99%)
    pallas_call x1, Pallas kernels, local_fn(): pl.pallas_call(functools.partial(kernel, n_dev), out_shape=jax.ShapeDtype...  171 us

profile of v4, /device:TPU:21, one launch (start us, length us, event | category | flops | bytes accessed | tf_op | source)
XLA Modules:
  0.0 172.5 jit_solution(14922184550718311026)
XLA Ops:
  0.6 170.6 %pair_energies.1.rows_ref = f32[8,16]{1,0:T(8,128)} custom-call(bf16[16,2,160,672]{3,2,1,0:T(8,128)(2,1)} %bitcast.3, f32[16,32]{1,0:T(8,128)} %eps_hbm.1, s32[16,32]{1,0:T(8,128)} %act_hbm.1, f32[16,160]{1,0:T(8,128)} %vir_hbm.1), custom_call_target="tpu_custom_call" | custom-call | flops 18166579200 | bytes 13762560 | tf_op jit(solution)/shard_map/pair_energies/pallas_call | solution.py:243
  171.3 1.2 finish.1

commit v5 on v4

--- a/solution.py
+++ b/solution.py
@@ -116,8 +116,8 @@
             k_part = k_ref[part, part]
             return fold_rows_of(k_part * (2.0 * k_part - k_part.T) / (eps_pair - vir_sum[part, part]))
         k_ab, k_ba = k_ref[high, low], k_ref[low, high].T
-        mixed = (2.0 * (k_ab * (k_ab - k_ba) + k_ba * k_ba)) / (eps_pair - vir_sum[high, low])
-        return jnp.concatenate([same(low) + fold_rows_of(mixed), same(high)], axis=1)
+        mixed = (k_ab * (k_ab - k_ba) + k_ba * k_ba) / (eps_pair - vir_sum[high, low])
+        return jnp.concatenate([same(low) + 2.0 * fold_rows_of(mixed), same(high)], axis=1)
 
     def add_energies(slot, first, fresh):
         row = [jnp.zeros(acc.shape[2:], jnp.float32)] * n_loc

time: 173 us -> 173 us (level)
  no operation moved by 1% of the time
where the time goes in v5:
time: 173 us; the launch traced here: 172 us
  Pallas kernels  172 us (99%)
    pallas_call x1, Pallas kernels, local_fn(): pl.pallas_call(functools.partial(kernel, n_dev), out_shape=jax.ShapeDtype...  171 us

profile of v5, /device:TPU:21, one launch (start us, length us, event | category | flops | bytes accessed | tf_op | source)
XLA Modules:
  0.0 172.5 jit_solution(17425675399302580292)
XLA Ops:
  0.6 170.6 %pair_energies.1.rows_ref = f32[8,16]{1,0:T(8,128)} custom-call(bf16[16,2,160,672]{3,2,1,0:T(8,128)(2,1)} %bitcast.3, f32[16,32]{1,0:T(8,128)} %eps_hbm.1, s32[16,32]{1,0:T(8,128)} %act_hbm.1, f32[16,160]{1,0:T(8,128)} %vir_hbm.1), custom_call_target="tpu_custom_call" | custom-call | flops 18166579200 | bytes 13762560 | tf_op jit(solution)/shard_map/pair_energies/pallas_call | solution.py:243
  171.3 1.2 finish.1
